TPU v7x, 32 devices: a whole 2x2x4 slice. The times are simulated.
32 devices in a mesh: gx: 4 (over z), gy: 2 (over x), gz: 4 (over y, core).
Axes of the slice: x: 2, y: 2, z: 4, core: 2. Of those that a mesh axis runs over, the one named last changes fastest.
Arguments:
- amplitudes: float32 [2, 8388608], P(None, ('gx', 'gy', 'gz')), may hold values from -6 to 6
- couplings: float32 [23], replicated, may hold values from -1.2 to 1.2
- fields: float32 [23], replicated, may hold values from 0.3 to 1.2
Outputs:
- evolved: float32 [2, 8388608], P(None, ('gx', 'gy', 'gz'))
All inputs are finite; a program needn't handle non-finite values.
Results may differ from a plain program's by a relative error of at most 0.000098.
Values sent between devices are 32-bit elements; how exact they have to be, the bound alone decides.
A program may use at most 64 MiB of HBM per device.

v0:
```python
import functools
import math

import jax
import jax.numpy as jnp
from jax import lax
from jax.experimental import pallas as pl
from jax.experimental.pallas import tpu as pltpu
from jax.sharding import PartitionSpec as P

MESH = pl.DeviceIdType.MESH
AXES = ("gx", "gy", "gz")
LANES = 128
CHUNK_BITS = 3
LOW_BITS = 5
EXACT = lax.Precision.HIGHEST


def log2(size):
    return size.bit_length() - 1


def bits_set(value, first, last):
    total = jnp.zeros_like(value)
    for bit in range(first, last):
        total = total + ((value >> bit) & 1)
    return total


def swapped(value):
    rows = value.shape[0]
    even = lax.broadcasted_iota(jnp.int32, value.shape, 0) & 1 == 0
    return jnp.where(even, pltpu.roll(value, rows - 1, 0), pltpu.roll(value, 1, 0))


def kernel(sizes, qubits, couplings, fields, amp, out, held, state, landed, done, low_c, low_s, high_c, high_s, cosine, sine, rows_w, lanes_w, in_sem, out_sem, send_sem, recv_sem):
    rows_all = held.shape[0]
    chunks = 1 << CHUNK_BITS
    chunk = rows_all // chunks
    lane_bits = log2(LANES)
    local_bits = log2(rows_all // 2) + lane_bits
    chunk_low = local_bits - CHUNK_BITS
    low_top = lane_bits + LOW_BITS
    tile = 2 << LOW_BITS
    highs = rows_all // tile
    place = {axis: lax.axis_index(axis) for axis in AXES}
    device = jnp.int32(0)
    for axis in AXES:
        device = device * sizes[axis] + place[axis]

    stages = {axis: [] for axis in AXES}
    qubit = local_bits
    for axis in reversed(AXES):
        for bit in range(log2(sizes[axis])):
            stages[axis].append((axis, bit, qubit))
            qubit += 1
    far = list(reversed(stages["gx"]))
    near = stages["gy"] + list(reversed(stages["gz"]))
    turn = near[1::-1] + near[2:]
    half = (len(far) + 1) // 2
    plans = (far[:half] + near + far[half:], far[half:] + turn + far[:half])
    count = len(plans[0])

    def partner(axis, bit):
        return tuple(place[a] ^ (1 << bit) if a == axis else place[a] for a in AXES)

    loads = [pltpu.make_async_copy(amp.at[pl.ds(c * chunk, chunk)], held.at[pl.ds(c * chunk, chunk)], in_sem.at[c]) for c in range(chunks)]
    for load in loads:
        load.start()
    barrier = pltpu.get_barrier_semaphore()
    for axis, bit, _ in plans[0]:
        pl.semaphore_signal(barrier, inc=1, device_id=partner(axis, bit), device_id_type=MESH)

    for q in range(qubits):
        cosine[pl.ds(q, 1), :] = jnp.full((1, LANES), fields[q], jnp.float32)
    angles = cosine[...]
    cosine[...] = jnp.cos(angles)
    sine[...] = jnp.sin(angles)

    def angle_of(position, bonds):
        total = jnp.zeros(position.shape, jnp.float32)
        for q in bonds:
            parity = (position >> q ^ position >> ((q + 1) % qubits)) & 1
            total = total + couplings[q] * (1.0 - 2.0 * parity.astype(jnp.float32))
        return total

    row = lax.broadcasted_iota(jnp.int32, (2 * tile, LANES), 0)
    lane = lax.broadcasted_iota(jnp.int32, (2 * tile, LANES), 1)
    position = (device << local_bits) + ((row >> 1) << lane_bits) + lane
    turns = bits_set(position, 0, low_top) & 3
    low = angle_of(position, list(range(low_top)) + [qubits - 1]) + turns.astype(jnp.float32) * (math.pi / 2)
    low_c[...] = jnp.cos(low)
    low_s[...] = jnp.sin(low)
    high_row = lax.broadcasted_iota(jnp.int32, (highs, LANES), 0)
    position = (device << local_bits) + (high_row << low_top)
    turns = bits_set(position, low_top, qubits) & 3
    high = angle_of(position, range(low_top, qubits - 1)) + turns.astype(jnp.float32) * (math.pi / 2)
    high_c[...] = jnp.cos(high)
    high_s[...] = jnp.sin(high)

    for load in loads:
        load.wait()

    @pl.loop(0, chunk // 8)
    def _(step):
        sign = jnp.where(lax.broadcasted_iota(jnp.int32, (8, LANES), 0) & 1 == 0, 1.0, -1.0)
        at = pl.multiple_of(step * 8, 8)
        low_at = pl.multiple_of(lax.rem(step * 8, 2 * tile), 8)
        c_low = low_c[pl.ds(low_at, 8), :]
        s_low = low_s[pl.ds(low_at, 8), :]
        high_at = step * 8 // tile
        parts = []
        for c in range(chunks):
            number = c * (chunk // tile) + high_at
            c_high = high_c[pl.ds(number, 1), :]
            s_high = high_s[pl.ds(number, 1), :]
            value = held[pl.ds(pl.multiple_of(c * chunk + at, 8), 8), :]
            c_all = c_low * c_high - s_low * s_high
            s_all = s_low * c_high + c_low * s_high
            parts.append(value * c_all + swapped(value) * (s_all * sign))
        for bit in range(CHUNK_BITS):
            c_q = cosine[pl.ds(chunk_low + bit, 1), :]
            s_q = sine[pl.ds(chunk_low + bit, 1), :]
            mixed = list(parts)
            for c in range(chunks):
                if not c >> bit & 1:
                    first, second = parts[c], parts[c | 1 << bit]
                    mixed[c] = c_q * first + s_q * second
                    mixed[c | 1 << bit] = s_q * first - c_q * second
            parts = mixed
        for c in range(chunks):
            state[0, pl.ds(pl.multiple_of(c * chunk + at, 8), 8), :] = parts[c]

    def send(c, k):
        axis, bit, _ = plans[c % 2][k]
        span = pl.ds(c * chunk, chunk)
        return pltpu.make_async_remote_copy(
            src_ref=state.at[k, span],
            dst_ref=landed.at[k, span],
            send_sem=send_sem.at[k, c],
            recv_sem=recv_sem.at[k, c],
            device_id=partner(axis, bit),
            device_id_type=MESH,
        )

    pl.semaphore_wait(barrier, count)
    for c in range(chunks):
        send(c, 0).start()

    def matrix(shape, first_row, skip, first, last):
        there = lax.broadcasted_iota(jnp.int32, shape, 0) + first_row
        here = lax.broadcasted_iota(jnp.int32, shape, 1)
        total = jnp.ones(shape, jnp.float32)
        if skip:
            total = jnp.where((there ^ here) & ((1 << skip) - 1) == 0, total, 0.0)
        repeat = shape[1] // LANES
        for q in range(first, last):
            bit = q - first + skip
            c_q = jnp.concatenate([cosine[pl.ds(q, 1), :]] * repeat, axis=1)
            s_q = jnp.concatenate([sine[pl.ds(q, 1), :]] * repeat, axis=1)
            up, left = there >> bit & 1, here >> bit & 1
            total = total * jnp.where(up ^ left == 1, s_q, jnp.where(up == 1, -c_q, c_q))
        return total

    lanes_w[...] = matrix((LANES, LANES), 0, 0, 0, lane_bits)

    @pl.loop(0, chunk // 8)
    def _(step):
        at = pl.multiple_of(step * 8, 8)
        rows_w[pl.ds(at, 8), :] = matrix((8, chunk), at, 1, lane_bits, chunk_low)

    block = LANES

    def local(c, source, target):
        @pl.loop(0, chunk // block)
        def _(step):
            at = pl.multiple_of(c * chunk + step * block, block)
            source[pl.ds(at, block), :] = jnp.dot(source[pl.ds(at, block), :], lanes_w[...], precision=EXACT, preferred_element_type=jnp.float32)

        @pl.loop(0, chunk // block)
        def _(step):
            at = pl.multiple_of(step * block, block)
            target[pl.ds(pl.multiple_of(c * chunk + at, block), block), :] = jnp.dot(
                rows_w[pl.ds(at, block), :], source[pl.ds(c * chunk, chunk), :], precision=EXACT, preferred_element_type=jnp.float32
            )

    def combine(c, k, target, last):
        axis, bit, q = plans[c % 2][k]
        own = 1.0 - 2.0 * ((place[axis] >> bit) & 1).astype(jnp.float32)

        @pl.loop(0, chunk // tile)
        def _(step):
            at = pl.multiple_of(c * chunk + step * tile, tile)
            c_q = cosine[pl.ds(q, 1), :] * own
            s_q = sine[pl.ds(q, 1), :]
            value = c_q * state[k, pl.ds(at, tile), :] + s_q * landed[k, pl.ds(at, tile), :]
            if last:
                row = lax.broadcasted_iota(jnp.int32, (tile, LANES), 0)
                lane = lax.broadcasted_iota(jnp.int32, (tile, LANES), 1)
                inner = ((row >> 1) << lane_bits) + lane
                number = (device << local_bits) + ((c * (chunk // tile) + step) << low_top)
                turns = bits_set(inner, 0, low_top) + bits_set(number, low_top, qubits)
                value = jnp.where(turns & 1 == 1, swapped(value), value)
                value = jnp.where((turns + (row & 1)) & 2 == 2, -value, value)
            target[pl.ds(at, tile), :] = value

    events = [(c // 2 + 0.5 * k if k < count - 1 else 2 * chunks + c // 2, k, c) for c in range(chunks) for k in range(count)]
    stores = []
    for _, k, c in sorted(events):
        send(c, k).wait_recv()
        if k == count - 1:
            combine(c, k, done, True)
            span = pl.ds(c * chunk, chunk)
            stores.append(pltpu.make_async_copy(done.at[span], out.at[span], out_sem.at[c]))
            stores[-1].start()
        elif k == 0:
            combine(c, k, done, False)
            local(c, done, state.at[1])
            send(c, 1).start()
        else:
            combine(c, k, state.at[k + 1], False)
            send(c, k + 1).start()
    for k in range(count):
        for c in range(chunks):
            send(c, k).wait_send()
    for store in stores:
        store.wait()


def solution(mesh):
    sizes = {axis: mesh.shape[axis] for axis in AXES}
    count = sum(log2(size) for size in sizes.values())

    def step(amplitudes, couplings, fields):
        local = amplitudes.shape[1]
        qubits = couplings.shape[0]
        rows = 2 * local // LANES
        chunks = 1 << CHUNK_BITS
        chunk = rows // chunks
        tile = 2 << LOW_BITS
        table = -(-qubits // 8) * 8
        woven = amplitudes.reshape(2, local // LANES, LANES).transpose(1, 0, 2).reshape(rows, LANES)
        vmem = lambda *shape: pltpu.VMEM(shape, jnp.float32)
        result = pl.pallas_call(
            functools.partial(kernel, sizes, qubits),
            out_shape=jax.ShapeDtypeStruct((rows, LANES), jnp.float32),
            in_specs=[pl.BlockSpec(memory_space=pltpu.SMEM)] * 2 + [pl.BlockSpec(memory_space=pl.ANY)],
            out_specs=pl.BlockSpec(memory_space=pl.ANY),
            scratch_shapes=[
                vmem(rows, LANES),
                vmem(count, rows, LANES),
                vmem(count, rows, LANES),
                vmem(rows, LANES),
                vmem(2 * tile, LANES),
                vmem(2 * tile, LANES),
                vmem(rows // tile, LANES),
                vmem(rows // tile, LANES),
                vmem(table, LANES),
                vmem(table, LANES),
                vmem(chunk, chunk),
                vmem(LANES, LANES),
                pltpu.SemaphoreType.DMA((chunks,)),
                pltpu.SemaphoreType.DMA((chunks,)),
                pltpu.SemaphoreType.DMA((count, chunks)),
                pltpu.SemaphoreType.DMA((count, chunks)),
            ],
            compiler_params=pltpu.CompilerParams(
                collective_id=0, has_side_effects=True, vmem_limit_bytes=60 << 20
            ),
        )(couplings, fields, woven)
        return result.reshape(local // LANES, 2, LANES).transpose(1, 0, 2).reshape(2, local)

    placed = (P(None, AXES), P(), P())
    return jax.shard_map(step, mesh=mesh, in_specs=placed, out_specs=P(None, AXES), check_vma=False)
```

profile of v0, /device:TPU:0, one launch (start us, length us, event | category | flops | bytes accessed | tf_op | source)
XLA Modules:
  0.0 102.4 jit_solution(18253677291349992270)
XLA Ops:
  0.0 99.8 %shard_map.37 = f32[4096,128]{1,0:T(8,128)} custom-call(f32[23]{0:T(128)} %couplings.1, f32[23]{0:T(128)} %fields.1, f32[4096,128]{1,0:T(8,128)} %bitcast.11), custom_call_target="tpu_custom_call" | custom-call | tf_op jit(solution)/shard_map/pallas_call | solution.py:244
  99.8 2.6 %copy.7 = f32[2,262144]{1,0:T(2,128)} copy(f32[2,262144]{1,0:T(2,128)} %bitcast.10) | data formatting | bytes 4194304
where the time goes:
time: 103 us; the launch traced here: 102 us
  Pallas kernels  99.8 us (97%)
  local copies, waits for them, and re-layouts  2.61 us (3%)
    pallas_call x1, Pallas kernels, step(): pl.pallas_call(functools.partial(kernel, sizes, qubits), out_shape=jax.Sh...  99.8 us
    unnamed x1, local copies, waits for them, and re-layouts  2.61 us

commit v1 on v0

--- a/solution.py
+++ b/solution.py
@@ -13,6 +13,7 @@
 LANES = 128
 CHUNK_BITS = 3
 LOW_BITS = 5
+VMEM = 67043328
 EXACT = lax.Precision.HIGHEST
 
 
@@ -33,7 +34,7 @@
     return jnp.where(even, pltpu.roll(value, rows - 1, 0), pltpu.roll(value, 1, 0))
 
 
-def kernel(sizes, qubits, couplings, fields, amp, out, held, state, landed, done, low_c, low_s, high_c, high_s, cosine, sine, rows_w, lanes_w, in_sem, out_sem, send_sem, recv_sem):
+def kernel(sizes, qubits, couplings, fields, amp, done, held, state, landed, low_c, low_s, high_c, high_s, cosine, sine, rows_w, lanes_w, in_sem, send_sem, recv_sem):
     rows_all = held.shape[0]
     chunks = 1 << CHUNK_BITS
     chunk = rows_all // chunks
@@ -205,14 +206,10 @@
             target[pl.ds(at, tile), :] = value
 
     events = [(c // 2 + 0.5 * k if k < count - 1 else 2 * chunks + c // 2, k, c) for c in range(chunks) for k in range(count)]
-    stores = []
     for _, k, c in sorted(events):
         send(c, k).wait_recv()
         if k == count - 1:
             combine(c, k, done, True)
-            span = pl.ds(c * chunk, chunk)
-            stores.append(pltpu.make_async_copy(done.at[span], out.at[span], out_sem.at[c]))
-            stores[-1].start()
         elif k == 0:
             combine(c, k, done, False)
             local(c, done, state.at[1])
@@ -223,8 +220,6 @@
     for k in range(count):
         for c in range(chunks):
             send(c, k).wait_send()
-    for store in stores:
-        store.wait()
 
 
 def solution(mesh):
@@ -243,14 +238,13 @@
         vmem = lambda *shape: pltpu.VMEM(shape, jnp.float32)
         result = pl.pallas_call(
             functools.partial(kernel, sizes, qubits),
-            out_shape=jax.ShapeDtypeStruct((rows, LANES), jnp.float32),
-            in_specs=[pl.BlockSpec(memory_space=pltpu.SMEM)] * 2 + [pl.BlockSpec(memory_space=pl.ANY)],
-            out_specs=pl.BlockSpec(memory_space=pl.ANY),
+            out_shape=pltpu.VMEM((rows, LANES), jnp.float32),
+            in_specs=[pl.BlockSpec(memory_space=pltpu.SMEM)] * 2 + [pl.BlockSpec(memory_space=pltpu.HBM)],
+            out_specs=pl.BlockSpec(memory_space=pltpu.VMEM),
             scratch_shapes=[
                 vmem(rows, LANES),
                 vmem(count, rows, LANES),
                 vmem(count, rows, LANES),
-                vmem(rows, LANES),
                 vmem(2 * tile, LANES),
                 vmem(2 * tile, LANES),
                 vmem(rows // tile, LANES),
@@ -260,12 +254,11 @@
                 vmem(chunk, chunk),
                 vmem(LANES, LANES),
                 pltpu.SemaphoreType.DMA((chunks,)),
-                pltpu.SemaphoreType.DMA((chunks,)),
                 pltpu.SemaphoreType.DMA((count, chunks)),
                 pltpu.SemaphoreType.DMA((count, chunks)),
             ],
             compiler_params=pltpu.CompilerParams(
-                collective_id=0, has_side_effects=True, vmem_limit_bytes=60 << 20
+                collective_id=0, has_side_effects=True, vmem_limit_bytes=VMEM - 4 * rows * LANES
             ),
         )(couplings, fields, woven)
         return result.reshape(local // LANES, 2, LANES).transpose(1, 0, 2).reshape(2, local)

time: 103 us -> 101 us (0.981)
  local copies, waits for them, and re-layouts: 2.61 us -> 1.32 us
    unnamed x1, local copies, waits for them, and re-layouts: 2.61 us -> 1.32 us
where the time goes in v1:
time: 101 us; the launch traced here: 100 us
  Pallas kernels  99 us (98%)
  local copies, waits for them, and re-layouts  1.32 us (1%)
    pallas_call x1, Pallas kernels, step(): pl.pallas_call(functools.partial(kernel, sizes, qubits), out_shape=pltpu....  99 us

profile of v1, /device:TPU:0, one launch (start us, length us, event | category | flops | bytes accessed | tf_op | source)
XLA Modules:
  0.0 100.4 jit_solution(17943519344569394253)
XLA Ops:
  0.0 99.0 %shard_map.37 = f32[4096,128]{1,0:T(8,128)S(1)} custom-call(f32[23]{0:T(128)} %couplings.1, f32[23]{0:T(128)} %fields.1, f32[4096,128]{1,0:T(8,128)} %bitcast.11), custom_call_target="tpu_custom_call" | custom-call | tf_op jit(solution)/shard_map/pallas_call | solution.py:239
  99.1 1.3 %copy.7 = f32[2,262144]{1,0:T(2,128)} copy(f32[2,262144]{1,0:T(2,128)S(1)} %bitcast.10) | data formatting | bytes 4194304

commit v2 on v1

--- a/solution.py
+++ b/solution.py
@@ -34,7 +34,7 @@
     return jnp.where(even, pltpu.roll(value, rows - 1, 0), pltpu.roll(value, 1, 0))
 
 
-def kernel(sizes, qubits, couplings, fields, amp, done, held, state, landed, low_c, low_s, high_c, high_s, cosine, sine, rows_w, lanes_w, in_sem, send_sem, recv_sem):
+def kernel(sizes, qubits, couplings, fields, amp, done, held, state, landed, low_c, low_s, high_c, high_s, cosine, sine, rows_w, lanes_w, in_sem, send_sem, recv_sem, far_send, far_recv):
     rows_all = held.shape[0]
     chunks = 1 << CHUNK_BITS
     chunk = rows_all // chunks
@@ -55,22 +55,29 @@
         for bit in range(log2(sizes[axis])):
             stages[axis].append((axis, bit, qubit))
             qubit += 1
-    far = list(reversed(stages["gx"]))
     near = stages["gy"] + list(reversed(stages["gz"]))
-    turn = near[1::-1] + near[2:]
-    half = (len(far) + 1) // 2
-    plans = (far[:half] + near + far[half:], far[half:] + turn + far[:half])
-    count = len(plans[0])
+    plans = (near, near[1::-1] + near[2:])
+    count = len(near)
+    parts_gx = sizes["gx"]
+    far_bits = log2(parts_gx)
+    part = chunk // parts_gx
+    part_low = chunk_low - far_bits
+    own = place["gx"]
 
     def partner(axis, bit):
         return tuple(place[a] ^ (1 << bit) if a == axis else place[a] for a in AXES)
+
+    def distant(apart):
+        return tuple(place[a] ^ apart if a == "gx" else place[a] for a in AXES)
 
     loads = [pltpu.make_async_copy(amp.at[pl.ds(c * chunk, chunk)], held.at[pl.ds(c * chunk, chunk)], in_sem.at[c]) for c in range(chunks)]
     for load in loads:
         load.start()
     barrier = pltpu.get_barrier_semaphore()
-    for axis, bit, _ in plans[0]:
+    for axis, bit, _ in near:
         pl.semaphore_signal(barrier, inc=1, device_id=partner(axis, bit), device_id_type=MESH)
+    for apart in range(1, parts_gx):
+        pl.semaphore_signal(barrier, inc=1, device_id=distant(apart), device_id_type=MESH)
 
     for q in range(qubits):
         cosine[pl.ds(q, 1), :] = jnp.full((1, LANES), fields[q], jnp.float32)
@@ -101,6 +108,19 @@
 
     for load in loads:
         load.wait()
+
+    def mix(parts, qubit):
+        for bit in range(log2(len(parts))):
+            c_q = cosine[pl.ds(qubit + bit, 1), :]
+            s_q = sine[pl.ds(qubit + bit, 1), :]
+            mixed = list(parts)
+            for p in range(len(parts)):
+                if not p >> bit & 1:
+                    first, second = parts[p], parts[p | 1 << bit]
+                    mixed[p] = c_q * first + s_q * second
+                    mixed[p | 1 << bit] = s_q * first - c_q * second
+            parts = mixed
+        return parts
 
     @pl.loop(0, chunk // 8)
     def _(step):
@@ -119,21 +139,12 @@
             c_all = c_low * c_high - s_low * s_high
             s_all = s_low * c_high + c_low * s_high
             parts.append(value * c_all + swapped(value) * (s_all * sign))
-        for bit in range(CHUNK_BITS):
-            c_q = cosine[pl.ds(chunk_low + bit, 1), :]
-            s_q = sine[pl.ds(chunk_low + bit, 1), :]
-            mixed = list(parts)
-            for c in range(chunks):
-                if not c >> bit & 1:
-                    first, second = parts[c], parts[c | 1 << bit]
-                    mixed[c] = c_q * first + s_q * second
-                    mixed[c | 1 << bit] = s_q * first - c_q * second
-            parts = mixed
+        parts = mix(parts, chunk_low)
         for c in range(chunks):
             state[0, pl.ds(pl.multiple_of(c * chunk + at, 8), 8), :] = parts[c]
 
     def send(c, k):
-        axis, bit, _ = plans[c % 2][k]
+        axis, bit, _ = plans[c % 2][k - 1]
         span = pl.ds(c * chunk, chunk)
         return pltpu.make_async_remote_copy(
             src_ref=state.at[k, span],
@@ -144,31 +155,55 @@
             device_id_type=MESH,
         )
 
-    pl.semaphore_wait(barrier, count)
+    def cross(c, apart, back):
+        theirs = pl.ds(pl.multiple_of(c * chunk + (own ^ apart) * part, 8), part)
+        mine = pl.ds(pl.multiple_of(c * chunk + own * part, 8), part)
+        return pltpu.make_async_remote_copy(
+            src_ref=state.at[count + 1 if back else 0, theirs],
+            dst_ref=done.at[mine] if back else landed.at[0, mine],
+            send_sem=far_send.at[back, apart, c],
+            recv_sem=far_recv.at[back, apart, c],
+            device_id=distant(apart),
+            device_id_type=MESH,
+        )
+
+    def premix(c):
+        @pl.loop(0, part // 8)
+        def _(step):
+            spans = [pl.ds(pl.multiple_of(c * chunk + p * part + step * 8, 8), 8) for p in range(parts_gx)]
+            for span, value in zip(spans, mix([state[0, span, :] for span in spans], part_low)):
+                state[0, span, :] = value
+
+    premix(0)
+    pl.semaphore_wait(barrier, count + parts_gx - 1)
     for c in range(chunks):
-        send(c, 0).start()
-
-    def matrix(shape, first_row, skip, first, last):
+        if c:
+            premix(c)
+        for apart in reversed(range(1, parts_gx)):
+            cross(c, apart, 0).start()
+
+    def matrix(shape, first_row, skip, kept):
         there = lax.broadcasted_iota(jnp.int32, shape, 0) + first_row
         here = lax.broadcasted_iota(jnp.int32, shape, 1)
         total = jnp.ones(shape, jnp.float32)
         if skip:
             total = jnp.where((there ^ here) & ((1 << skip) - 1) == 0, total, 0.0)
         repeat = shape[1] // LANES
-        for q in range(first, last):
-            bit = q - first + skip
+        for bit, q in enumerate(kept, skip):
             c_q = jnp.concatenate([cosine[pl.ds(q, 1), :]] * repeat, axis=1)
             s_q = jnp.concatenate([sine[pl.ds(q, 1), :]] * repeat, axis=1)
             up, left = there >> bit & 1, here >> bit & 1
             total = total * jnp.where(up ^ left == 1, s_q, jnp.where(up == 1, -c_q, c_q))
         return total
 
-    lanes_w[...] = matrix((LANES, LANES), 0, 0, 0, lane_bits)
+    lanes_w[...] = matrix((LANES, LANES), 0, 0, range(lane_bits))
+
+    inside = list(range(lane_bits, part_low)) + list(range(qubits - far_bits, qubits))
 
     @pl.loop(0, chunk // 8)
     def _(step):
         at = pl.multiple_of(step * 8, 8)
-        rows_w[pl.ds(at, 8), :] = matrix((8, chunk), at, 1, lane_bits, chunk_low)
+        rows_w[pl.ds(at, 8), :] = matrix((8, chunk), at, 1, inside)
 
     block = LANES
 
@@ -185,46 +220,57 @@
                 rows_w[pl.ds(at, block), :], source[pl.ds(c * chunk, chunk), :], precision=EXACT, preferred_element_type=jnp.float32
             )
 
-    def combine(c, k, target, last):
-        axis, bit, q = plans[c % 2][k]
-        own = 1.0 - 2.0 * ((place[axis] >> bit) & 1).astype(jnp.float32)
+    def combine(c, k, last):
+        axis, bit, q = plans[c % 2][k - 1]
+        side = 1.0 - 2.0 * ((place[axis] >> bit) & 1).astype(jnp.float32)
 
         @pl.loop(0, chunk // tile)
         def _(step):
             at = pl.multiple_of(c * chunk + step * tile, tile)
-            c_q = cosine[pl.ds(q, 1), :] * own
+            c_q = cosine[pl.ds(q, 1), :] * side
             s_q = sine[pl.ds(q, 1), :]
             value = c_q * state[k, pl.ds(at, tile), :] + s_q * landed[k, pl.ds(at, tile), :]
             if last:
-                row = lax.broadcasted_iota(jnp.int32, (tile, LANES), 0)
+                row = lax.broadcasted_iota(jnp.int32, (tile, LANES), 0) + step * tile
                 lane = lax.broadcasted_iota(jnp.int32, (tile, LANES), 1)
-                inner = ((row >> 1) << lane_bits) + lane
-                number = (device << local_bits) + ((c * (chunk // tile) + step) << low_top)
-                turns = bits_set(inner, 0, low_top) + bits_set(number, low_top, qubits)
+                owner = row // part
+                home = c * chunk + own * part + row - owner * part
+                turns = bits_set((home >> 1 << lane_bits) + lane, 0, local_bits)
+                turns = turns + bits_set(owner, 0, far_bits) + bits_set(device & (1 << count) - 1, 0, count)
                 value = jnp.where(turns & 1 == 1, swapped(value), value)
                 value = jnp.where((turns + (row & 1)) & 2 == 2, -value, value)
-            target[pl.ds(at, tile), :] = value
-
-    events = [(c // 2 + 0.5 * k if k < count - 1 else 2 * chunks + c // 2, k, c) for c in range(chunks) for k in range(count)]
-    for _, k, c in sorted(events):
-        send(c, k).wait_recv()
-        if k == count - 1:
-            combine(c, k, done, True)
-        elif k == 0:
-            combine(c, k, done, False)
-            local(c, done, state.at[1])
-            send(c, 1).start()
+            state[k + 1, pl.ds(at, tile), :] = value
+
+    for _, k, c in sorted((c + k, k, c) for c in range(chunks) for k in range(count + 1)):
+        mine = pl.ds(pl.multiple_of(c * chunk + own * part, 8), part)
+        if k == 0:
+            landed[0, mine, :] = state[0, mine, :]
+            for apart in range(1, parts_gx):
+                cross(c, apart, 0).wait_recv()
+            local(c, landed.at[0], state.at[1])
         else:
-            combine(c, k, state.at[k + 1], False)
+            send(c, k).wait_recv()
+            combine(c, k, k == count)
+        if k < count:
             send(c, k + 1).start()
-    for k in range(count):
-        for c in range(chunks):
+        else:
+            for apart in reversed(range(1, parts_gx)):
+                cross(c, apart, 1).start()
+            done[mine, :] = state[count + 1, mine, :]
+    for c in range(chunks):
+        for k in range(1, count + 1):
             send(c, k).wait_send()
+        for apart in range(1, parts_gx):
+            cross(c, apart, 0).wait_send()
+            cross(c, apart, 1).wait_send()
+    for c in range(chunks):
+        for apart in range(1, parts_gx):
+            cross(c, apart, 1).wait_recv()
 
 
 def solution(mesh):
     sizes = {axis: mesh.shape[axis] for axis in AXES}
-    count = sum(log2(size) for size in sizes.values())
+    count = log2(sizes["gy"]) + log2(sizes["gz"])
 
     def step(amplitudes, couplings, fields):
         local = amplitudes.shape[1]
@@ -243,8 +289,8 @@
             out_specs=pl.BlockSpec(memory_space=pltpu.VMEM),
             scratch_shapes=[
                 vmem(rows, LANES),
-                vmem(count, rows, LANES),
-                vmem(count, rows, LANES),
+                vmem(count + 2, rows, LANES),
+                vmem(count + 1, rows, LANES),
                 vmem(2 * tile, LANES),
                 vmem(2 * tile, LANES),
                 vmem(rows // tile, LANES),
@@ -254,8 +300,10 @@
                 vmem(chunk, chunk),
                 vmem(LANES, LANES),
                 pltpu.SemaphoreType.DMA((chunks,)),
-                pltpu.SemaphoreType.DMA((count, chunks)),
-                pltpu.SemaphoreType.DMA((count, chunks)),
+                pltpu.SemaphoreType.DMA((count + 1, chunks)),
+                pltpu.SemaphoreType.DMA((count + 1, chunks)),
+                pltpu.SemaphoreType.DMA((2, sizes["gx"], chunks)),
+                pltpu.SemaphoreType.DMA((2, sizes["gx"], chunks)),
             ],
             compiler_params=pltpu.CompilerParams(
                 collective_id=0, has_side_effects=True, vmem_limit_bytes=VMEM - 4 * rows * LANES

time: 101 us -> 106 us (1.050)
  Pallas kernels: 99 us -> 104 us
    pallas_call x1, Pallas kernels: 99 us -> 104 us  [step(): pl.pallas_call(functools.partial(kernel, sizes, qubits), out_shape=pltpu....]
where the time goes in v2:
time: 106 us
  Pallas kernels  104 us (98%)
  local copies, waits for them, and re-layouts  1.32 us (1%)
    pallas_call x1, Pallas kernels, step(): pl.pallas_call(functools.partial(kernel, sizes, qubits), out_shape=pltpu....  104 us

profile of v2, /device:TPU:0, one launch (start us, length us, event | category | flops | bytes accessed | tf_op | source)
XLA Modules:
  0.0 105.8 jit_solution(10343641229542015017)
XLA Ops:
  0.0 104.5 %shard_map.37 = f32[4096,128]{1,0:T(8,128)S(1)} custom-call(f32[23]{0:T(128)} %couplings.1, f32[23]{0:T(128)} %fields.1, f32[4096,128]{1,0:T(8,128)} %bitcast.11), custom_call_target="tpu_custom_call" | custom-call | tf_op jit(solution)/shard_map/pallas_call | solution.py:285
  104.5 1.3 %copy.7 = f32[2,262144]{1,0:T(2,128)} copy(f32[2,262144]{1,0:T(2,128)S(1)} %bitcast.10) | data formatting | bytes 4194304
